TPU v7x, 32 devices: a whole 2x2x4 slice. The times are simulated.
32 devices in a mesh: data: 8 (over z, y), pipe: 4 (over x, core).
Axes of the slice: x: 2, y: 2, z: 4, core: 2. Of those that a mesh axis runs over, the one named last changes fastest.
Arguments:
- acts_in: bfloat16 [192, 64, 512], P(('data', 'pipe'))
- cot_out: bfloat16 [192, 64, 512], P(('data', 'pipe'))
- seq_lens: int32 [192], P(('data', 'pipe'))
- w_qkv: bfloat16 [4, 512, 1536], P('pipe')
- w_out: bfloat16 [4, 8, 64, 512], P('pipe')
- w_up: bfloat16 [4, 512, 2048], P('pipe')
- w_down: bfloat16 [4, 2048, 512], P('pipe')
- gain_attn: bfloat16 [4, 512], P('pipe')
- gain_mlp: bfloat16 [4, 512], P('pipe')
Outputs:
- output 1: bfloat16 [192, 64, 512], P(('data', 'pipe'))
- output 2: float32 [4, 512, 1536], P('pipe')
- output 3: float32 [4, 8, 64, 512], P('pipe')
- output 4: float32 [4, 512, 2048], P('pipe')
- output 5: float32 [4, 2048, 512], P('pipe')
- output 6: float32 [4, 512], P('pipe')
- output 7: float32 [4, 512], P('pipe')
All inputs are finite; a program needn't handle non-finite values.
Results may differ from a plain program's by a relative error of at most 0.02.
Values are sent between devices in bfloat16 or wider.
A program may use at most 1 GiB of HBM per device.

v0:
```python
import functools
import jax
import jax.numpy as jnp
from jax import lax
from jax.experimental import pallas as pl
from jax.experimental.pallas import tpu as pltpu
from jax.sharding import PartitionSpec as P

NORM_EPS = 1e-5
MESH = pl.DeviceIdType.MESH
F32 = jnp.float32
BF16 = jnp.bfloat16
SEQ = 64
HEAD = 64
D = 512
FFN = 2048
PIPE = 4
DATA = 8
LINE = 4
TILE = 128
PART_B = 64
UNITS_A = 30
EXTRA = 5
UNITS_X = UNITS_A // EXTRA
SLOTS = 4
SEQ_MB = 4
PAIRS = 4


def dot_nn(lhs, rhs):
    return lax.dot_general(lhs, rhs, (((1,), (0,)), ((), ())), preferred_element_type=F32)


def dot_nt(lhs, rhs):
    return lax.dot_general(lhs, rhs, (((1,), (1,)), ((), ())), preferred_element_type=F32)


def dot_tn(lhs, rhs):
    return lax.dot_general(lhs, rhs, (((0,), (0,)), ((), ())), preferred_element_type=F32)


def pass_kernel(n_seq, acts_ref, cot_ref, lens_ref, wqkv_hbm, wout_hbm, wup_hbm, wdown_hbm, ga_ref, gm_ref,
                out_ref, gp_s, gain_ref,
                wqkv, wout, wup, wdown, lens_buf, xin, cin, hout, na_s, qkv_s, ctx_s, mid_s, nm_s, gelu_s,
                dpre_s, dmid_s, p_s, s_scr, gain_acc, gain_all, ya_buf, la_buf, ra_buf, yb_buf, lb_buf, rb_buf, yx_buf, lx_buf, rx_buf,
                ya_out, la_out, ra_out, yb_out, lb_out, rb_out, yx_out, lx_out, rx_out,
                w_sem, in_sem, x_sem, c_sem, len_sem, send_sem, home_sem, sum_recv, sum_send, part_send, gain_recv, gain_send):
    pos = lax.axis_index('pipe')
    rep = lax.axis_index('data')
    rep_z, rep_y = rep // 2, rep % 2
    n_tok = n_seq * SEQ
    n_mb = n_seq // SEQ_MB
    n_own = n_seq // PIPE
    own_slab = pl.ds(pos * n_own, n_own)
    for seq in range(n_own):
        lens_buf[pos * n_own + seq] = jnp.full((8, 128), lens_ref[seq], jnp.int32)
    last = PIPE - 1

    w_copies = [pltpu.make_async_copy(src, dst, w_sem.at[idx]) for idx, (src, dst) in enumerate(
        ((wqkv_hbm, wqkv), (wout_hbm, wout), (wup_hbm, wup), (wdown_hbm, wdown)))]
    for w_copy in w_copies:
        w_copy.start()

    barrier = pltpu.get_barrier_semaphore()
    for step in range(1, PIPE):
        pl.semaphore_signal(barrier, inc=1, device_id={'pipe': (pos + step) % PIPE}, device_id_type=MESH)
    for step in range(1, DATA):
        pl.semaphore_signal(barrier, inc=1, device_id={'data': (rep + step) % DATA}, device_id_type=MESH)
    pl.semaphore_wait(barrier, PIPE - 1 + DATA - 1)

    def first_seq(mb, size):
        return mb * size

    def rows_of(mb, size):
        return pl.ds(pl.multiple_of(first_seq(mb, size) * SEQ, SEQ), size * SEQ)

    def seq_rows(mb, size, seq):
        return pl.ds(pl.multiple_of((first_seq(mb, size) + seq) * SEQ, SEQ), SEQ)

    def part_rows(mb, size, part):
        return pl.ds(pl.multiple_of(part * n_tok + first_seq(mb, size) * SEQ, SEQ), size * SEQ)

    def send_to(src, dst, send, recv, target):
        pltpu.make_async_remote_copy(src_ref=src, dst_ref=dst, send_sem=send, recv_sem=recv,
                                     device_id={'pipe': target}, device_id_type=MESH).start()

    def place(src, dst, send, recv, target):
        @pl.when(target == pos)
        def _():
            pltpu.make_async_copy(src, dst, recv).start()

        @pl.when(target != pos)
        def _():
            send_to(src, dst, send, recv, target)

    for step in range(1, PIPE):
        send_to(lens_buf.at[own_slab], lens_buf.at[own_slab], in_sem.at[step - 1], len_sem.at[pos], (pos + step) % PIPE)
    spread = []
    for src, dst, sem, target in ((acts_ref, xin, x_sem, 0), (cot_ref, cin, c_sem, last)):
        for seq in range(n_own):
            at = pos * n_own + seq
            mb = at // SEQ_MB
            spread.append((src.at[pl.ds(seq * SEQ, SEQ)], dst.at[pl.ds(pl.multiple_of(at * SEQ, SEQ), SEQ)],
                           in_sem.at[PIPE - 1 + len(spread)], sem.at[mb], target))
    for item in spread:
        place(*item)

    lane = lax.broadcasted_iota(jnp.int32, (SEQ, 128), 1)
    row = lax.broadcasted_iota(jnp.int32, (SEQ, 128), 0)
    first = lane < HEAD
    key_pos = jnp.where(first, lane, lane - HEAD)
    lane_row = lax.broadcasted_iota(jnp.int32, (1, 128), 1)
    take_a = jnp.where(lane_row < HEAD, 1.0, 0.0).astype(BF16)
    take_b = jnp.where(lane_row < HEAD, 0.0, 1.0).astype(BF16)

    def blocks(pair_cols):
        return jnp.concatenate([pair_cols * take_a, pair_cols * take_b], axis=0)

    def halves_sum(arr):
        sum_a = jnp.sum(jnp.where(first[None], arr, 0.0), axis=-1, keepdims=True)
        sum_b = jnp.sum(jnp.where(first[None], 0.0, arr), axis=-1, keepdims=True)
        return sum_a, sum_b

    def lens_of(mb, size, seq):
        return lens_buf[first_seq(mb, size) + seq][0:1, :]

    def valid_mask(lens_row):
        ok = jnp.where(row < lens_row, 1.0, 0.0)
        return jnp.concatenate([ok] * (D // 128), axis=1)

    def inv_rms(val):
        return lax.rsqrt(jnp.mean(val * val, axis=-1, keepdims=True) + NORM_EPS)

    def forward(size, mb, _):
        rows = rows_of(mb, size)
        start = first_seq(mb, size)

        for home in range(PIPE):
            @pl.when((mb == home * n_own // size) & (home != pos))
            def _(home=home):
                slab = lens_buf.at[pl.ds(home * n_own, n_own)]
                pltpu.make_async_copy(slab, slab, len_sem.at[home]).wait()

        x_view = xin.at[rows]
        pltpu.make_async_copy(x_view, x_view, x_sem.at[mb]).wait()
        gain_a = ga_ref[...].astype(F32)
        hid = xin[rows, :].astype(F32)
        normed = (hid * inv_rms(hid) * gain_a).astype(BF16)
        na_s[rows, :] = normed
        for part in range(3):
            cols = slice(part * D, (part + 1) * D)
            qkv_s[rows, cols] = dot_nn(normed, wqkv[:, cols]).astype(BF16)

        for seq in range(size):
            for pair in range(PAIRS):
                q_cols = qkv_s[seq_rows(mb, size, seq), pair * 128:(pair + 1) * 128]
                k_cols = qkv_s[seq_rows(mb, size, seq), D + pair * 128:D + (pair + 1) * 128]
                spot = (seq * PAIRS + pair) * SEQ
                s_scr[spot:spot + SEQ, :] = dot_nt(q_cols, blocks(k_cols))
        for seq in range(size):
            visible = (key_pos <= row) & (key_pos < lens_of(mb, size, seq))
            spot = seq * PAIRS * SEQ
            scores = s_scr[spot:spot + PAIRS * SEQ, :].reshape(PAIRS, SEQ, 128) * (HEAD ** -0.5)
            scores = jnp.where(visible[None], scores, -1e30)
            max_a = jnp.max(jnp.where(first[None], scores, -3e38), axis=-1, keepdims=True)
            max_b = jnp.max(jnp.where(first[None], -3e38, scores), axis=-1, keepdims=True)
            expd = jnp.exp(scores - jnp.where(first[None], max_a, max_b))
            sum_a, sum_b = halves_sum(expd)
            probs = expd * jnp.where(first[None], 1.0 / sum_a, 1.0 / sum_b)
            p_rows = pl.ds(pl.multiple_of(start * PAIRS * SEQ + spot, SEQ), PAIRS * SEQ)
            p_s[p_rows, :] = probs.reshape(PAIRS * SEQ, 128)
        for seq in range(size):
            for pair in range(PAIRS):
                v_cols = qkv_s[seq_rows(mb, size, seq), 2 * D + pair * 128:2 * D + (pair + 1) * 128]
                p_rows = pl.ds(pl.multiple_of((start * PAIRS + seq * PAIRS + pair) * SEQ, SEQ), SEQ)
                ctx_s[seq_rows(mb, size, seq), pair * 128:(pair + 1) * 128] = dot_nn(
                    p_s[p_rows, :].astype(BF16), blocks(v_cols)).astype(BF16)
        mid = (hid + dot_nn(ctx_s[rows, :], wout[...])).astype(BF16)
        mid_s[rows, :] = mid
        mid_f = mid.astype(F32)
        normed_m = (mid_f * inv_rms(mid_f) * gm_ref[...].astype(F32)).astype(BF16)
        nm_s[rows, :] = normed_m
        for part in range(FFN // D):
            cols = slice(part * D, (part + 1) * D)
            pre = dot_nn(normed_m, wup[:, cols])
            cdf = 0.5 + 0.5 * lax.erf(pre * (0.5 ** 0.5))
            gelu_s[rows, cols] = (pre * cdf).astype(BF16)
            gp_s[part_rows(mb, size, part), :] = cdf + pre * (jnp.exp(pre * pre * -0.5) * 0.3989422804014327)
        top = mid_f + dot_nn(gelu_s[rows, :], wdown[...])
        for seq in range(size):
            mask = valid_mask(jnp.where(pos == last, lens_of(mb, size, seq), SEQ))
            piece = top[seq * SEQ:(seq + 1) * SEQ, :].astype(BF16)
            hout[seq_rows(mb, size, seq), :] = jnp.where(mask > 0.0, piece.astype(F32), 0.0).astype(BF16)

        h_view = hout.at[rows]

        @pl.when(pos < last)
        def _():
            send_to(h_view, xin.at[rows], send_sem.at[mb], x_sem.at[mb], pos + 1)

        @pl.when(pos == last)
        def _():
            for seq in range(size):
                at = start + seq
                home = at // n_own
                s_view = hout.at[seq_rows(mb, size, seq)]
                o_view = out_ref.at[pl.ds(pl.multiple_of((at % n_own) * SEQ, SEQ), SEQ)]

                @pl.when(home == pos)
                def _(s_view=s_view, o_view=o_view):
                    pltpu.make_async_copy(s_view, o_view, send_sem.at[mb]).start()

                @pl.when(home != pos)
                def _(s_view=s_view, o_view=o_view, home=home):
                    send_to(s_view, o_view, send_sem.at[mb], home_sem, home)

        return 0

    for w_copy in w_copies:
        w_copy.wait()
    lax.fori_loop(0, n_mb, functools.partial(forward, SEQ_MB), 0)

    def sent(size, mb, _):
        h_view = hout.at[rows_of(mb, size)]
        pltpu.make_async_copy(h_view, h_view, send_sem.at[mb]).wait()
        return 0

    gain_acc[...] = jnp.zeros_like(gain_acc)

    def norm_back(hid, gain, d_normed):
        inv = inv_rms(hid)
        unit = hid * inv
        d_gain = jnp.sum((d_normed * unit).reshape(hid.shape[0] // 8, 8, D), axis=0)
        scaled = d_normed * gain
        return inv * (scaled - unit * jnp.mean(unit * scaled, axis=-1, keepdims=True)), d_gain

    def backward(size, mb, _):
        rows = rows_of(mb, size)
        start = first_seq(mb, size)
        c_view = cin.at[rows]
        pltpu.make_async_copy(c_view, c_view, c_sem.at[mb]).wait()

        for seq in range(size):
            mask = valid_mask(lens_of(mb, size, seq))
            cin[seq_rows(mb, size, seq), :] = jnp.where(mask > 0.0, cin[seq_rows(mb, size, seq), :].astype(F32), 0.0).astype(BF16)
        d_top = cin[rows, :]
        for part in range(FFN // D):
            cols = slice(part * D, (part + 1) * D)
            d_gelu = dot_nt(d_top, wdown[cols, :])
            dpre_s[rows, cols] = (d_gelu * gp_s[part_rows(mb, size, part), :]).astype(BF16)
        d_nm = dot_nt(dpre_s[rows, :], wup[...])
        d_add, d_gain = norm_back(mid_s[rows, :].astype(F32), gm_ref[...].astype(F32), d_nm)
        gain_acc[1] += d_gain
        d_mid = d_top.astype(F32) + d_add
        d_mid_bf = d_mid.astype(BF16)
        dmid_s[rows, :] = d_mid_bf
        d_ctx = dot_nt(d_mid_bf, wout[...]).astype(BF16)
        for seq in range(size):
            for pair in range(PAIRS):
                v_cols = qkv_s[seq_rows(mb, size, seq), 2 * D + pair * 128:2 * D + (pair + 1) * 128]
                dc = d_ctx[seq * SEQ:(seq + 1) * SEQ, pair * 128:(pair + 1) * 128]
                spot = (seq * PAIRS + pair) * SEQ
                p_rows = pl.ds(pl.multiple_of(start * PAIRS * SEQ + spot, SEQ), SEQ)
                s_scr[spot:spot + SEQ, :] = dot_nt(dc, blocks(v_cols))
                both = dot_tn(p_s[p_rows, :].astype(BF16), dc)
                qkv_s[seq_rows(mb, size, seq), 2 * D + pair * 128:2 * D + (pair + 1) * 128] = jnp.where(
                    first, both[:SEQ], both[SEQ:]).astype(BF16)
        for seq in range(size):
            spot = seq * PAIRS * SEQ
            p_rows = pl.ds(pl.multiple_of(start * PAIRS * SEQ + spot, SEQ), PAIRS * SEQ)
            probs = p_s[p_rows, :].reshape(PAIRS, SEQ, 128)
            d_probs = s_scr[spot:spot + PAIRS * SEQ, :].reshape(PAIRS, SEQ, 128)
            sum_a, sum_b = halves_sum(probs * d_probs)
            d_scores = probs * (d_probs - jnp.where(first[None], sum_a, sum_b)) * (HEAD ** -0.5)
            s_scr[spot:spot + PAIRS * SEQ, :] = d_scores.reshape(PAIRS * SEQ, 128)
        for seq in range(size):
            for pair in range(PAIRS):
                q_at = slice(pair * 128, (pair + 1) * 128)
                k_at = slice(D + pair * 128, D + (pair + 1) * 128)
                q_cols = qkv_s[seq_rows(mb, size, seq), q_at]
                k_cols = qkv_s[seq_rows(mb, size, seq), k_at]
                spot = (seq * PAIRS + pair) * SEQ
                d_sc = s_scr[spot:spot + SEQ, :].astype(BF16)
                both = dot_tn(d_sc, q_cols)
                qkv_s[seq_rows(mb, size, seq), q_at] = dot_nn(d_sc, blocks(k_cols)).astype(BF16)
                qkv_s[seq_rows(mb, size, seq), k_at] = jnp.where(first, both[:SEQ], both[SEQ:]).astype(BF16)
        d_na = dot_nt(qkv_s[rows, :], wqkv[...])
        d_add, d_gain = norm_back(xin[rows, :].astype(F32), ga_ref[...].astype(F32), d_na)
        gain_acc[0] += d_gain

        @pl.when(pos > 0)
        def _():
            sent(size, mb, 0)
            hout[rows, :] = (d_mid + d_add).astype(BF16)
            send_to(hout.at[rows], cin.at[rows], send_sem.at[mb], c_sem.at[mb], pos - 1)

        return 0

    lax.fori_loop(0, n_mb, functools.partial(backward, SEQ_MB), 0)

    gain_all[rep] = jnp.concatenate([jnp.sum(gain_acc[0], axis=0, keepdims=True), jnp.sum(gain_acc[1], axis=0, keepdims=True),
                                     jnp.zeros((6, D), F32)], axis=0)
    for step in range(1, DATA):
        pltpu.make_async_remote_copy(src_ref=gain_all.at[rep], dst_ref=gain_all.at[rep], send_sem=gain_send,
                                     recv_sem=gain_recv.at[rep], device_id={'data': (rep + step) % DATA},
                                     device_id_type=MESH).start()

    per_tile = TILE // PART_B
    n_down, n_up, n_qkv = FFN // TILE, (D // TILE) * (FFN // D), (D // TILE) * 3

    def tile_kinds(tile):
        up, qkv, out = tile - n_down, tile - n_down - n_up, tile - n_down - n_up - n_qkv
        return (
            (tile < n_down, gelu_s, cin, tile, 0),
            ((up >= 0) & (qkv < 0), nm_s, dpre_s, up // (FFN // D), up % (FFN // D)),
            ((qkv >= 0) & (out < 0), na_s, qkv_s, qkv // 3, qkv % 3),
            (out >= 0, ctx_s, dmid_s, out, 0),
        )

    def tile_at(tile):
        return pl.ds(pl.multiple_of(tile * TILE, TILE), TILE)

    def compute_tile(tile):
        for cond, lhs, rhs, at_row, at_col in tile_kinds(tile):
            @pl.when(cond)
            def _(lhs=lhs, rhs=rhs, at_row=at_row, at_col=at_col):
                cols = pl.ds(0, D) if rhs.shape[1] == D else pl.ds(pl.multiple_of(at_col * D, D), D)
                gp_s[tile_at(tile), :] = dot_tn(lhs[:, pl.ds(pl.multiple_of(at_row * TILE, TILE), TILE)], rhs[:, cols])

    to_y, to_right, to_left = rep + 1 - 2 * rep_y, rep + 2, rep - 2

    def part_done(src, colour, link, slot):
        pltpu.make_async_copy(src, src, part_send.at[colour, link, slot]).wait()

    def ship_part(unit, slot, src, dst, colour, link, target, value):
        @pl.when(unit >= SLOTS)
        def _():
            part_done(src, colour, link, slot)

        src[...] = value
        pltpu.make_async_remote_copy(src_ref=src, dst_ref=dst, send_sem=part_send.at[colour, link, slot],
                                     recv_sem=sum_recv.at[colour, link, slot], device_id={'data': target},
                                     device_id_type=MESH).start()

    def ship(src, dst, link, recv, target):
        pltpu.make_async_remote_copy(src_ref=src, dst_ref=dst, send_sem=sum_send.at[link], recv_sem=recv,
                                     device_id={'data': target}, device_id_type=MESH).start()

    def arrived(view, recv):
        pltpu.make_async_copy(view, view, recv).wait()

    def gp_rows(start, size):
        return pl.ds(pl.multiple_of(start, 8), size)

    def line_actions(zz, colour, block, size, buf_l, buf_r, out_l, out_r, hop_rs, hop_ag):
        chunk = size // LINE
        own, above = zz * chunk, (zz + 1) * chunk

        def rs_right(unit, slot):
            at = block(unit)
            if zz > 0:
                arrived(buf_l.at[slot, own:size], sum_recv.at[colour, 1, slot])
                gp_s[gp_rows(at + own, chunk), :] += buf_l[slot, own:above, :]
            if zz < LINE - 1:
                value = gp_s[gp_rows(at + above, size - above), :]
                if zz > 0:
                    value = value + buf_l[slot, above:size, :]
                ship_part(unit, slot, out_r.at[slot, above:size], buf_l.at[slot, above:size], colour, 1, to_right, value)

        def rs_left(unit, slot):
            at = block(unit)
            if zz < LINE - 1:
                arrived(buf_r.at[slot, 0:above], sum_recv.at[colour, 2, slot])
                gp_s[gp_rows(at + own, chunk), :] += buf_r[slot, own:above, :]
            if zz > 0:
                value = gp_s[gp_rows(at, own), :]
                if zz < LINE - 1:
                    value = value + buf_r[slot, 0:own, :]
                ship_part(unit, slot, out_l.at[slot, 0:own], buf_r.at[slot, 0:own], colour, 2, to_left, value)

        def ag_right(unit, slot):
            at = block(unit)
            if zz > 0:
                arrived(gp_s.at[gp_rows(at, own)], sum_recv.at[colour, 3, slot])
            if zz < LINE - 1:
                view = gp_s.at[gp_rows(at, above)]
                ship(view, view, 1, sum_recv.at[colour, 3, slot], to_right)

        def ag_left(unit, slot):
            at = block(unit)
            if zz < LINE - 1:
                arrived(gp_s.at[gp_rows(at + above, size - above)], sum_recv.at[colour, 4, slot])
            if zz > 0:
                view = gp_s.at[gp_rows(at + own, size - own)]
                ship(view, view, 2, sum_recv.at[colour, 4, slot], to_left)

        return ([(hop_rs + zz, rs_right), (hop_rs + LINE - 1 - zz, rs_left)],
                [(hop_ag + zz, ag_right), (hop_ag + LINE - 1 - zz, ag_left)])

    half_a, part_b = TILE // 2, PART_B // LINE
    half_b = part_b // 2

    def actions_a(zz):
        def mine(unit):
            return unit * TILE + rep_y * half_a

        def theirs(unit):
            return unit * TILE + (1 - rep_y) * half_a

        def y_send(unit, slot):
            ship_part(unit, slot, ya_out.at[slot], ya_buf.at[slot], 0, 0, to_y, gp_s[gp_rows(theirs(unit), half_a), :])

        def y_add(unit, slot):
            arrived(ya_buf.at[slot], sum_recv.at[0, 0, slot])
            gp_s[gp_rows(mine(unit), half_a), :] += ya_buf[slot]

        def y_give(unit, slot):
            view = gp_s.at[gp_rows(mine(unit), half_a)]
            ship(view, view, 0, sum_recv.at[0, 5, slot], to_y)

        def finish(unit, slot):
            arrived(gp_s.at[gp_rows(theirs(unit), half_a)], sum_recv.at[0, 5, slot])

        scatter, gather = line_actions(zz, 0, mine, half_a, la_buf, ra_buf, la_out, ra_out, 1, 4)
        return [(0, y_send), (1, y_add)] + scatter + gather + [(7, y_give), (8, finish)]

    def actions_b(zz, colour, base, bufs, outs):
        y_buf, l_buf, r_buf = bufs
        y_out, l_out, r_out = outs

        def block(unit):
            return UNITS_A * TILE + (base + unit) * PART_B

        def mine(unit):
            return block(unit) + zz * part_b + rep_y * half_b

        def theirs(unit):
            return block(unit) + zz * part_b + (1 - rep_y) * half_b

        def y_send(unit, slot):
            ship_part(unit, slot, y_out.at[slot], y_buf.at[slot], colour, 0, to_y, gp_s[gp_rows(theirs(unit), half_b), :])

        def y_add(unit, slot):
            arrived(y_buf.at[slot], sum_recv.at[colour, 0, slot])
            gp_s[gp_rows(mine(unit), half_b), :] += y_buf[slot]
            view = gp_s.at[gp_rows(mine(unit), half_b)]
            ship(view, view, 0, sum_recv.at[colour, 5, slot], to_y)

        def y_done(unit, slot):
            arrived(gp_s.at[gp_rows(theirs(unit), half_b)], sum_recv.at[colour, 5, slot])

        scatter, gather = line_actions(zz, colour, block, PART_B, l_buf, r_buf, l_out, r_out, 0, 5)
        return scatter + [(3, y_send), (4, y_add), (5, y_done)] + gather

    def unit_of(colour, tick):
        inside = (tick >= 0) & (tick < UNITS_A)
        if colour < 2:
            return inside, tick
        return inside & (tick % EXTRA == 0), tick // EXTRA

    def run_actions(tick, hops):
        for zz in range(LINE):
            @pl.when(rep_z == zz)
            def _(zz=zz):
                todo = (
                    actions_a(zz),
                    actions_b(zz, 1, 0, (yb_buf, lb_buf, rb_buf), (yb_out, lb_out, rb_out)),
                    actions_b(zz, 2, UNITS_A, (yx_buf, lx_buf, rx_buf), (yx_out, lx_out, rx_out)),
                )
                for want in hops:
                    for colour in range(3):
                        fns = [fn for hop, fn in todo[colour] if hop == want]
                        if not fns:
                            continue
                        fresh, unit = unit_of(colour, tick - want)

                        @pl.when(fresh)
                        def _(fns=fns, unit=unit):
                            for fn in fns:
                                fn(unit, unit % SLOTS)

    def compute_for(tick):
        @pl.when(tick < UNITS_A)
        def _():
            compute_tile(tick)

        for colour, base in ((1, 0), (2, UNITS_A)):
            fresh, unit = unit_of(colour, tick)

            @pl.when(fresh & (unit % per_tile == 0))
            def _(unit=unit, base=base):
                compute_tile(UNITS_A + (base + unit) // per_tile)

    compute_for(0)

    def tick_step(tick, _):
        run_actions(tick, [0])
        compute_for(tick + 1)
        run_actions(tick, range(1, 9))
        return 0

    lax.fori_loop(0, UNITS_A + 8, tick_step, 0)

    def sent_all(link, size):
        view = gp_s.at[pl.ds(0, size)]
        pltpu.make_async_copy(view, view, sum_send.at[link]).wait()

    for zz in range(LINE):
        @pl.when(rep_z == zz)
        def _(zz=zz):
            line_rows = UNITS_A * (half_a // LINE) + (UNITS_A + UNITS_X) * part_b
            sent_all(0, UNITS_A * half_a + (UNITS_A + UNITS_X) * half_b)
            if zz < LINE - 1:
                sent_all(1, line_rows * (zz + 1))
            if zz > 0:
                sent_all(2, line_rows * (LINE - zz))
            for slot in range(SLOTS):
                for colour, (out_y, out_l, out_r) in enumerate(
                        ((ya_out, la_out, ra_out), (yb_out, lb_out, rb_out), (yx_out, lx_out, rx_out))):
                    size = out_l.shape[1]
                    part_done(out_y.at[slot], colour, 0, slot)
                    if zz < LINE - 1:
                        part_done(out_r.at[slot, (zz + 1) * size // LINE:size], colour, 1, slot)
                    if zz > 0:
                        part_done(out_l.at[slot, 0:zz * size // LINE], colour, 2, slot)

    for step in range(1, DATA):
        peer = (rep + step) % DATA
        pltpu.make_async_copy(gain_all.at[peer], gain_all.at[peer], gain_recv.at[peer]).wait()
    total = gain_all[0]
    for peer in range(1, DATA):
        total = total + gain_all[peer]
    gain_ref[...] = total
    pltpu.make_async_copy(gain_all.at[pl.ds(0, DATA - 1)], gain_all.at[pl.ds(0, DATA - 1)], gain_send).wait()

    lax.fori_loop(0, n_mb, functools.partial(sent, SEQ_MB), 0)

    @pl.when(pos < last)
    def _():
        pltpu.make_async_copy(out_ref, out_ref, home_sem).wait()

    for step in range(1, PIPE):
        pltpu.make_async_copy(lens_buf.at[own_slab], lens_buf.at[own_slab], in_sem.at[step - 1]).wait()
    for src, _, send, _, target in spread:
        @pl.when(target != pos)
        def _(src=src, send=send):
            pltpu.make_async_copy(src, src, send).wait()


def run_pass(acts, cots, lens, w_qkv, w_out, w_up, w_down, gain_a, gain_m):
    n_tok = acts.shape[0] * PIPE
    n_seq = n_tok // SEQ
    n_mb = n_seq // SEQ_MB
    any_spec = pl.BlockSpec(memory_space=pl.ANY)
    vmem_spec = pl.BlockSpec(memory_space=pltpu.VMEM)
    dma = pltpu.SemaphoreType.DMA
    return pl.pallas_call(
        functools.partial(pass_kernel, n_seq),
        out_shape=(
            pltpu.VMEM(acts.shape, BF16),
            pltpu.VMEM((n_tok * FFN // D, D), F32),
            pltpu.VMEM((8, D), F32),
        ),
        in_specs=[any_spec] * 2 + [pl.BlockSpec(memory_space=pltpu.SMEM)] + [any_spec] * 4 + [vmem_spec] * 2,
        out_specs=[vmem_spec] * 3,
        scratch_shapes=[
            pltpu.VMEM((D, 3 * D), BF16),
            pltpu.VMEM((D, D), BF16),
            pltpu.VMEM((D, FFN), BF16),
            pltpu.VMEM((FFN, D), BF16),
            pltpu.VMEM((n_seq, 8, 128), jnp.int32),
            pltpu.VMEM((n_tok, D), BF16),
            pltpu.VMEM((n_tok, D), BF16),
            pltpu.VMEM((n_tok, D), BF16),
            pltpu.VMEM((n_tok, D), BF16),
            pltpu.VMEM((n_tok, 3 * D), BF16),
            pltpu.VMEM((n_tok, D), BF16),
            pltpu.VMEM((n_tok, D), BF16),
            pltpu.VMEM((n_tok, D), BF16),
            pltpu.VMEM((n_tok, FFN), BF16),
            pltpu.VMEM((n_tok, FFN), BF16),
            pltpu.VMEM((n_tok, D), BF16),
            pltpu.VMEM((n_tok * PAIRS, 128), F32),
            pltpu.VMEM((SEQ_MB * PAIRS * SEQ, 128), F32),
            pltpu.VMEM((2, 8, D), F32),
            pltpu.VMEM((DATA, 8, D), F32),
        ] + [
            pltpu.VMEM((SLOTS, size, D), F32)
            for size in ((TILE // 2,) * 3 + (PART_B // LINE // 2, PART_B, PART_B) * 2) * 2
        ] + [
            dma((4,)),
            dma((2 * (n_seq // PIPE) + PIPE - 1,)),
            dma((n_mb,)),
            dma((n_mb,)),
            dma((PIPE,)),
            dma((n_mb,)),
            dma,
            dma((3, 6, SLOTS)),
            dma((3,)),
            dma((3, 3, SLOTS)),
            dma((DATA,)),
            dma,
        ],
        compiler_params=pltpu.CompilerParams(collective_id=0, has_side_effects=True, vmem_limit_bytes=50 * 1024 * 1024),
    )(acts, cots, lens, w_qkv, w_out, w_up, w_down, gain_a, gain_m)


def write_kernel(acts_ref, tiles_ref, gain_ref, out_ref, gqkv_ref, gout_ref, gup_ref, gdown_ref, gga_ref, ggm_ref,
                 out_sem, put_sem):
    give = pltpu.make_async_copy(acts_ref, out_ref, out_sem)
    give.start()
    row = 0
    dsts = (gdown_ref, gup_ref, gqkv_ref, gout_ref)
    for dst in dsts:
        for at_row in range(0, dst.shape[0], TILE):
            for at_col in range(0, dst.shape[1], D):
                pltpu.make_async_copy(tiles_ref.at[row:row + TILE], dst.at[at_row:at_row + TILE, at_col:at_col + D],
                                      put_sem).start()
                row += TILE
    gga_ref[...] = gain_ref[0:1, :]
    ggm_ref[...] = gain_ref[1:2, :]
    give.wait()
    pltpu.make_async_copy(tiles_ref, tiles_ref, put_sem).wait()


def write_out(acts, tiles, gains):
    any_spec = pl.BlockSpec(memory_space=pl.ANY)
    vmem_spec = pl.BlockSpec(memory_space=pltpu.VMEM)
    dma = pltpu.SemaphoreType.DMA
    return pl.pallas_call(
        write_kernel,
        out_shape=(
            jax.ShapeDtypeStruct(acts.shape, BF16),
            jax.ShapeDtypeStruct((D, 3 * D), F32),
            jax.ShapeDtypeStruct((D, D), F32),
            jax.ShapeDtypeStruct((D, FFN), F32),
            jax.ShapeDtypeStruct((FFN, D), F32),
            jax.ShapeDtypeStruct((1, D), F32),
            jax.ShapeDtypeStruct((1, D), F32),
        ),
        in_specs=[any_spec, any_spec, vmem_spec],
        out_specs=[any_spec] * 5 + [vmem_spec] * 2,
        scratch_shapes=[dma, dma],
        compiler_params=pltpu.CompilerParams(vmem_limit_bytes=4 * 1024 * 1024),
    )(acts, tiles, gains)


def solution(mesh):
    row_spec = P(('data', 'pipe'))
    stage_spec = P('pipe')

    def device_pass(acts_in, cot_out, seq_lens, w_qkv, w_out, w_up, w_down, gain_attn, gain_mlp):
        outs = run_pass(acts_in.reshape(-1, D), cot_out.reshape(-1, D), seq_lens, w_qkv.reshape(D, 3 * D),
                        w_out.reshape(D, D), w_up.reshape(D, FFN), w_down.reshape(FFN, D),
                        gain_attn, gain_mlp)
        acts_out, g_qkv, g_out, g_up, g_down, g_ga, g_gm = write_out(*outs)
        grads = (g_qkv.reshape(w_qkv.shape), g_out.reshape(w_out.shape), g_up.reshape(w_up.shape), g_down.reshape(w_down.shape),
                 g_ga, g_gm)
        return (acts_out.reshape(acts_in.shape),) + grads

    return jax.shard_map(device_pass, mesh=mesh, in_specs=(row_spec, row_spec, row_spec) + (stage_spec,) * 6, out_specs=(row_spec,) + (stage_spec,) * 6, check_vma=False)
```

profile of v0, /device:TPU:0, one launch (start us, length us, event | category | flops | bytes accessed | tf_op | source)
XLA Modules:
  0.0 315.4 jit_solution(7742609367813001195)
XLA Ops:
  0.6 309.5 %shard_map.144 = (bf16[384,512]{1,0:T(8,128)(2,1)S(1)}, f32[6144,512]{1,0:T(8,128)S(1)}, f32[8,512]{1,0:T(8,128)S(1)}) custom-call(bf16[384,512]{1,0:T(8,128)(2,1)} %bitcast.15, bf16[384,512]{1,0:T(8,128)(2,1)} %bitcast.16, s32[6]{0:T(128)} %lens_ref.1, bf16[512,1536]{1,0:T(8,128)(2,1)} %bitcast.13, bf16[512,512]{1,0:T(8,128)(2,1)} %bitcast.14, ...), custom_call_target="tpu_custom_call" | custom-call | tf_op jit(solution)/shard_map/pallas_call | solution.py:557
  310.2 5.2 %shard_map.145 = (bf16[384,512]{1,0:T(8,128)(2,1)}, f32[512,1536]{1,0:T(8,128)}, f32[512,512]{1,0:T(8,128)}, f32[512,2048]{1,0:T(8,128)}, f32[2048,512]{1,0:T(8,...) custom-call(bf16[384,512]{1,0:T(8,128)(2,1)S(1)} %get-tuple-element.17.acts_ref, f32[6144,512]{1,0:T(8,128)S(1)} %get-tuple-element.18.tiles_ref, ...), custom_call_target="tpu_custom_call" | custom-call | tf_op jit(solution)/shard_map/pallas_call | solution.py:630
where the time goes:
time: 316 us; the launch traced here: 315 us
  Pallas kernels  315 us (100%)
    pallas_call x1, Pallas kernels, run_pass(): pl.pallas_call(functools.partial(pass_kernel, n_seq), out_shape=(pltpu.VM...  310 us

commit v1 on v0

--- a/solution.py
+++ b/solution.py
@@ -23,7 +23,7 @@
 EXTRA = 5
 UNITS_X = UNITS_A // EXTRA
 SLOTS = 4
-SEQ_MB = 4
+SEQ_MB = 6
 PAIRS = 4
 
 

time: 316 us -> 324 us (1.025)
  Pallas kernels: 315 us -> 323 us
    pallas_call x1, Pallas kernels: 310 us -> 317 us  [run_pass(): pl.pallas_call(functools.partial(pass_kernel, n_seq), out_shape=(pltpu.VM...]
where the time goes in v1:
time: 324 us
  Pallas kernels  323 us (100%)
    pallas_call x1, Pallas kernels, run_pass(): pl.pallas_call(functools.partial(pass_kernel, n_seq), out_shape=(pltpu.VM...  317 us

profile of v1, /device:TPU:0, one launch (start us, length us, event | category | flops | bytes accessed | tf_op | source)
XLA Modules:
  0.0 323.5 jit_solution(2748375327324771668)
XLA Ops:
  0.6 317.5 %shard_map.144 = (bf16[384,512]{1,0:T(8,128)(2,1)S(1)}, f32[6144,512]{1,0:T(8,128)S(1)}, f32[8,512]{1,0:T(8,128)S(1)}) custom-call(bf16[384,512]{1,0:T(8,128)(2,1)} %bitcast.15, bf16[384,512]{1,0:T(8,128)(2,1)} %bitcast.16, s32[6]{0:T(128)} %lens_ref.1, bf16[512,1536]{1,0:T(8,128)(2,1)} %bitcast.13, bf16[512,512]{1,0:T(8,128)(2,1)} %bitcast.14, ...), custom_call_target="tpu_custom_call" | custom-call | tf_op jit(solution)/shard_map/pallas_call | solution.py:557
  318.1 5.2 %shard_map.145 = (bf16[384,512]{1,0:T(8,128)(2,1)}, f32[512,1536]{1,0:T(8,128)}, f32[512,512]{1,0:T(8,128)}, f32[512,2048]{1,0:T(8,128)}, f32[2048,512]{1,0:T(8,...) custom-call(bf16[384,512]{1,0:T(8,128)(2,1)S(1)} %get-tuple-element.17.acts_ref, f32[6144,512]{1,0:T(8,128)S(1)} %get-tuple-element.18.tiles_ref, ...), custom_call_target="tpu_custom_call" | custom-call | tf_op jit(solution)/shard_map/pallas_call | solution.py:630
